TPU v7x, 32 devices: a whole 2x2x4 slice. The times are simulated.
32 devices in a mesh: ctx: 8 (over z, core), tp: 4 (over y, x).
Axes of the slice: x: 2, y: 2, z: 4, core: 2. Of those that a mesh axis runs over, the one named last changes fastest.
Arguments:
- tokens: bfloat16 [2, 4096, 8192], P(None, 'ctx', 'tp'), may hold values from -14 to 14
- norm_gain: float32 [8192], replicated, may hold values from 0.5 to 1.5
- span_order: int32 [2, 16], replicated, may hold values from 0 to 15, each once within a row
- w_query: bfloat16 [8192, 4096], P('ctx', 'tp'), may hold values from -0.10122281 to 0.10122281
- w_key: bfloat16 [8192, 1024], P('ctx', 'tp'), may hold values from -0.10122281 to 0.10122281
- value_weight: bfloat16 [8192, 1024], P('ctx', 'tp'), may hold values from -0.0625 to 0.0625
- w_out: bfloat16 [4096, 8192], P('tp', 'ctx'), may hold values from -0.75 to 0.75
Outputs:
- mixed: bfloat16 [2, 4096, 8192], P(None, 'ctx', 'tp')
Inputs may be any that keep to these rules, and one draw needn't show every extreme that they name: Each row of span_order names every one of the 2 * 8 blocks of positions once; stored block b of a sequence holds positions span_order[b] * 256 onwards, in order.
All inputs are finite; a program needn't handle non-finite values.
Results may differ from a plain program's by a relative error of at most 0.014.
Values may be sent and summed in bfloat16 or wider, within the bound.
A program may use at most 128 MiB of HBM per device.

v0:
```python
import math
import jax
import jax.numpy as jnp
from jax import lax
from jax.sharding import PartitionSpec as P

HEAD_DIM = 128
theta_base = 500000.0
norm_eps = 1e-05
masked_score = -1e30


def normalize(flat_rows, norm_gain):
    wide = flat_rows.astype(jnp.float32)
    factor = lax.rsqrt(jnp.mean(wide * wide, axis=-1, keepdims=True) + norm_eps)
    return (wide * factor * norm_gain).astype(jnp.bfloat16)


def positions_of(span_order, first, count, block_rows):
    stored = first + jnp.arange(count, dtype=jnp.int32)
    which = stored // block_rows
    slots = jnp.arange(span_order.shape[1], dtype=jnp.int32)
    picked = jnp.sum(
        jnp.where(slots[None, None, :] == which[None, :, None], span_order[:, None, :], 0), axis=2
    )
    return picked * block_rows + stored % block_rows


def apply_rotation(value_rows, token_position, head_size):
    half = head_size // 2
    freqs = jnp.exp(-(2.0 * jnp.arange(half, dtype=jnp.float32) / head_size) * math.log(theta_base))
    angle = token_position.astype(jnp.float32)[..., None] * freqs
    cosine = jnp.cos(angle)[:, :, None, :]
    sine = jnp.sin(angle)[:, :, None, :]
    front = value_rows[..., :half]
    back = value_rows[..., half:]
    return jnp.concatenate([front * cosine - back * sine, back * cosine + front * sine], axis=-1)


def per_device(tokens, norm_gain, span_order, w_query, w_key, value_weight, w_out):
    sequence_batch, rows_dev, _ = tokens.shape
    head_size = HEAD_DIM
    query_heads = w_query.shape[1] // head_size
    key_heads = w_key.shape[1] // head_size
    group_width = query_heads // key_heads
    block_rows = rows_dev // 2
    total_rows = sequence_batch * rows_dev
    factor = 1.0 / math.sqrt(head_size)
    rank = lax.axis_index("ctx")
    whole = lax.all_gather(tokens, "tp", axis=2, tiled=True)
    normed = normalize(whole.reshape(total_rows, whole.shape[2]), norm_gain)
    query_pos = positions_of(span_order, rank * rows_dev, rows_dev, block_rows)
    latest = jnp.max(query_pos, axis=1)
    stat_shape = (sequence_batch, key_heads, group_width, rows_dev)
    initial = (
        jnp.full(stat_shape, masked_score, jnp.float32),
        jnp.zeros(stat_shape, jnp.float32),
        jnp.zeros(stat_shape + (head_size,), jnp.float32),
    )
    pieces = (
        lax.all_gather(w_query, "ctx", axis=0, tiled=True),
        lax.all_gather(w_key, "ctx", axis=0, tiled=True),
        lax.all_gather(value_weight, "ctx", axis=0, tiled=True),
    )
    query_flat, flattened_key, flattened_value = tuple(
        (jnp.dot(normed, piece, preferred_element_type=jnp.float32) for piece in pieces)
    )
    turned = apply_rotation(
        query_flat.reshape(sequence_batch, rows_dev, query_heads, head_size), query_pos, head_size
    ).astype(jnp.bfloat16)
    query = turned.reshape(sequence_batch, rows_dev, key_heads, group_width, head_size).transpose(
        0, 2, 3, 1, 4
    )
    turned = apply_rotation(
        flattened_key.reshape(sequence_batch, rows_dev, key_heads, head_size), query_pos, head_size
    ).astype(jnp.bfloat16)
    own_values = flattened_value.reshape(sequence_batch, rows_dev, key_heads, head_size).astype(
        jnp.bfloat16
    )
    key_piece = lax.all_gather(turned, "ctx", axis=1, tiled=True)
    value_piece = lax.all_gather(own_values, "ctx", axis=1, tiled=True)
    count = key_piece.shape[1]
    step_rows = 512

    def one_block(index, state):
        first = index * step_rows
        key_block = lax.dynamic_slice_in_dim(key_piece, first, step_rows, 1)
        value_block = lax.dynamic_slice_in_dim(value_piece, first, step_rows, 1)
        key_pos = positions_of(span_order, first, step_rows, block_rows)

        def update(current):
            peak, total, summed = current
            scores = (
                jnp.einsum(
                    "shgqd,skhd->shgqk", query, key_block, preferred_element_type=jnp.float32
                )
                * factor
            )
            allowed = key_pos[:, None, None, None, :] <= query_pos[:, None, None, :, None]
            scores = jnp.where(allowed, scores, masked_score)
            new_peak = jnp.maximum(peak, jnp.max(scores, axis=-1))
            weights = jnp.where(allowed, jnp.exp(scores - new_peak[..., None]), 0.0)
            shrink = jnp.exp(peak - new_peak)
            total = total * shrink + jnp.sum(weights, axis=-1)
            summed = summed * shrink[..., None] + jnp.einsum(
                "shgqk,skhd->shgqd",
                weights.astype(jnp.bfloat16),
                value_block,
                preferred_element_type=jnp.float32,
            )
            return (new_peak, total, summed)

        return lax.cond(
            jnp.all(jnp.min(key_pos, axis=1) > latest), lambda kept: kept, update, state
        )

    peak, total, summed = lax.fori_loop(0, count // step_rows, one_block, initial)
    attended = (summed / total[..., None]).astype(jnp.bfloat16)
    attended = attended.transpose(0, 3, 1, 2, 4).reshape(total_rows, query_heads * head_size)
    terms = jnp.dot(
        attended,
        lax.all_gather(w_out, "ctx", axis=1, tiled=True),
        preferred_element_type=jnp.float32,
    )
    mixed = lax.psum_scatter(terms.astype(jnp.bfloat16), "tp", scatter_dimension=1, tiled=True)
    return mixed.reshape(sequence_batch, rows_dev, mixed.shape[1])


def solution(mesh):
    placed = (
        P(None, "ctx", "tp"),
        P(),
        P(),
        P("ctx", "tp"),
        P("ctx", "tp"),
        P("ctx", "tp"),
        P("tp", "ctx"),
    )
    return jax.shard_map(
        per_device, mesh=mesh, in_specs=placed, out_specs=P(None, "ctx", "tp"), check_vma=False
    )
```

profile of v0, /device:TPU:0, one launch (start us, length us, event | category | flops | bytes accessed | tf_op | source)
XLA Modules:
  0.0 862.1 jit_solution(7252307660646929625)
XLA Ops:
  10.5 48.0 %all-gather.10.cloned.1.call-done = bf16[8192,256]{1,0:T(8,128)(2,1)} async-done(((bf16[1024,256]{1,0:T(8,128)(2,1)}), bf16[8192,256]{1,0:T(8,128)(2,1)}) %all-gather.10.cloned.1.call-update) | async-done | bytes 4194320 | tf_op jit(solution)/shard_map/all_gather | solution.py:62
  58.6 6.3 copy.24
  64.9 151.7 %all-gather.8.cloned.1.call-done = bf16[2,512,8192]{2,1,0:T(8,128)(2,1)} async-done(((bf16[2,512,2048]{2,1,0:T(8,128)(2,1)}), bf16[2,512,8192]{2,1,0:T(8,128)(2,1)}) %all-gather.8.cloned.1.call-update) | async-done | bytes 16777232 | tf_op jit(solution)/shard_map/all_gather | solution.py:50
  216.5 7.5 fusion.21
  224.0 9.0 %fusion.29 = f32[2,512,2,128]{1,3,2,0:T(8,128)S(1)} fusion(bf16[2,128,8192,1]{2,1,0,3:T(8,128)(2,1)S(1)} %bitcast.69, bf16[2,512,8192]{2,1,0:T(8,128)(2,1)} %all-gather.8.cloned.1.call-done, f32[8192]{0:T(1024)S(1)} %copy-done.2, f32[2,512]{1,0:T(2,128)S(1)} %add_rsqrt_fusion), kind=kOutput, calls=%fused_computation.49 | convolution fusion | flops 4328521728 | bytes 22056960 | tf_op jit(solution)/shard_map/dot_general | solution.py:66
  234.2 30.9 %all-gather.16.cloned.1.call-done = bf16[8192,256]{1,0:T(8,128)(2,1)} async-done(((bf16[1024,256]{1,0:T(8,128)(2,1)}), bf16[8192,256]{1,0:T(8,128)(2,1)}) %all-gather.16.cloned.1.call-update) | async-done | bytes 4194320 | tf_op jit(solution)/shard_map/all_gather | solution.py:63
  265.1 6.3 copy.28
  271.4 12.7 %convolution_convert_fusion.1 = bf16[2,512,2,128]{3,1,2,0:T(8,128)(2,1)} fusion(bf16[2,128,8192,1]{2,1,0,3:T(8,128)(2,1)} %bitcast.70, bf16[2,512,8192]{2,1,0:T(8,128)(2,1)} %all-gather.8.cloned.1.call-done, f32[8192]{0:T(1024)S(1)} %copy-done.2, f32[2,512]{1,0:T(2,128)S(1)} %add_rsqrt_fusion), kind=kOutput, calls=%fused_computation.47 | convolution fusion | flops 4328783872 | bytes 21532672 | tf_op jit(solution)/shard_map/dot_general | solution.py:66
  285.2 131.2 %all-gather.14.cloned.1.call-done = bf16[8192,1024]{1,0:T(8,128)(2,1)} async-done(((bf16[1024,1024]{1,0:T(8,128)(2,1)}), bf16[8192,1024]{1,0:T(8,128)(2,1)}) %all-gather.14.cloned.1.call-update) | async-done | bytes 16777232 | tf_op jit(solution)/shard_map/all_gather | solution.py:61
  416.4 21.4 %copy.25 = bf16[1024,8192]{1,0:T(8,128)(2,1)} copy(bf16[1024,8192]{0,1:T(8,128)(2,1)} %bitcast.63) | data formatting | bytes 33554432 | tf_op jit(solution)/shard_map/dot_general | solution.py:66
  437.9 22.4 %fusion.27 = f32[2,512,8,128]{1,3,2,0:T(8,128)S(1)} fusion(bf16[8,128,8192,1]{2,1,0,3:T(8,128)(2,1)} %bitcast.64, bf16[2,512,8192]{2,1,0:T(8,128)(2,1)} %all-gather.8.cloned.1.call-done, f32[8192]{0:T(1024)S(1)} %copy-done.2, f32[2,512]{1,0:T(2,128)S(1)} %add_rsqrt_fusion), kind=kOutput, calls=%fused_computation.48 | convolution fusion | flops 17213423616 | bytes 37785600 | tf_op jit(solution)/shard_map/dot_general | solution.py:66
  469.9 6.4 copy.29
  476.3 33.8 %all-gather.18.cloned.1.call-done = bf16[2,4096,2,128]{3,1,2,0:T(8,128)(2,1)} async-done(((bf16[2,512,2,128]{3,1,2,0:T(8,128)(2,1)}), bf16[2,4096,2,128]{3,1,2,0:T(8,128)(2,1)}) %all-gather.18.cloned.1.call-update) | async-done | bytes 4194320 | tf_op jit(solution)/shard_map/all_gather | solution.py:81
  512.6 156.1 %while.19 = (s32[]{:T(128)}, f32[2,2,4,512]{3,2,1,0:T(4,128)S(1)}, f32[2,2,4,512]{3,2,1,0:T(4,128)S(1)}, f32[2,2,4,512,128]{4,3,2,1,0:T(8,128)}, s32[2,16]{1,0:T...) while((s32[]{:T(128)}, f32[2,2,4,512]{3,2,1,0:T(4,128)S(1)}, ...), condition=%wide.region_11.12_spmd, body=%wide.region_3.11_spmd.sunk | while | flops 2204700672 | bytes 64532936 | solution.py:117
  514.2 17.9 %conditional.2 = (f32[2,2,4,512]{3,2,1,0:T(4,128)S(1)}, f32[2,2,4,512]{3,2,1,0:T(4,128)S(1)}, f32[2,2,4,512,128]{4,3,2,1,0:T(8,128)}) conditional(s32[]{:T(128)} %convert_element_type.85, (s32[2,512]{1,0:T(2,128)S(1)}, s32[2,512]{1,0:T(2,128)S(1)}, s32[]{:T(128)}, bf16[2,4096,2,128]{3,1,2,0:T(8,128)(2,1)}, bf16[2,2,4,512,128]{4,3,2,1,0:T(8,128)(2,1)}, ...), branch_computations={%region_7.9_spmd, %region_10.10_spmd} | conditional | flops 2204647424 | bytes 64430148 | solution.py:113
  514.6 4.7 fusion
  519.3 4.1 fusion.2
  523.5 8.7 %multiply_add_fusion = f32[2,2,4,512,128]{4,3,2,1,0:T(8,128)} fusion(f32[2,2,4,512,128]{4,3,2,1,0:T(8,128)} %get-tuple-element.360, f32[2,2,4,512]{3,2,1,0:T(4,128)S(1)} %bitcast.76, f32[2,2,512,4,512]{4,2,3,1,0:T(8,128)S(1)} %get-tuple-element.437, f32[2,2,4,512]{3,2,1,0:T(4,128)S(1)} %max.5, pred[2,512,512]{1,2,0:T(8,128)(4,1)S(1)} %broadcast_compare_fusion, ...), kind=kOutput, calls=%fused_computation.7 | convolution fusion | flops 1096810496 | bytes 26279940 | tf_op jit(solution)/shard_map/while/body/eval_jaxpr/cond/branch_0_fun/shgqk,skhd->shgqd/dot_general | solution.py:105
  533.8 17.9 %conditional.2 = (f32[2,2,4,512]{3,2,1,0:T(4,128)S(1)}, f32[2,2,4,512]{3,2,1,0:T(4,128)S(1)}, f32[2,2,4,512,128]{4,3,2,1,0:T(8,128)}) conditional(s32[]{:T(128)} %convert_element_type.85, (s32[2,512]{1,0:T(2,128)S(1)}, s32[2,512]{1,0:T(2,128)S(1)}, s32[]{:T(128)}, bf16[2,4096,2,128]{3,1,2,0:T(8,128)(2,1)}, bf16[2,2,4,512,128]{4,3,2,1,0:T(8,128)(2,1)}, ...), branch_computations={%region_7.9_spmd, %region_10.10_spmd} | conditional | flops 2204647424 | bytes 64430148 | solution.py:113
  534.2 4.7 fusion
  538.9 4.1 fusion.2
  543.0 8.7 %multiply_add_fusion = f32[2,2,4,512,128]{4,3,2,1,0:T(8,128)} fusion(f32[2,2,4,512,128]{4,3,2,1,0:T(8,128)} %get-tuple-element.360, f32[2,2,4,512]{3,2,1,0:T(4,128)S(1)} %bitcast.76, f32[2,2,512,4,512]{4,2,3,1,0:T(8,128)S(1)} %get-tuple-element.437, f32[2,2,4,512]{3,2,1,0:T(4,128)S(1)} %max.5, pred[2,512,512]{1,2,0:T(8,128)(4,1)S(1)} %broadcast_compare_fusion, ...), kind=kOutput, calls=%fused_computation.7 | convolution fusion | flops 1096810496 | bytes 26279940 | tf_op jit(solution)/shard_map/while/body/eval_jaxpr/cond/branch_0_fun/shgqk,skhd->shgqd/dot_general | solution.py:105
  553.3 17.9 %conditional.2 = (f32[2,2,4,512]{3,2,1,0:T(4,128)S(1)}, f32[2,2,4,512]{3,2,1,0:T(4,128)S(1)}, f32[2,2,4,512,128]{4,3,2,1,0:T(8,128)}) conditional(s32[]{:T(128)} %convert_element_type.85, (s32[2,512]{1,0:T(2,128)S(1)}, s32[2,512]{1,0:T(2,128)S(1)}, s32[]{:T(128)}, bf16[2,4096,2,128]{3,1,2,0:T(8,128)(2,1)}, bf16[2,2,4,512,128]{4,3,2,1,0:T(8,128)(2,1)}, ...), branch_computations={%region_7.9_spmd, %region_10.10_spmd} | conditional | flops 2204647424 | bytes 64430148 | solution.py:113
  553.7 4.7 fusion
  558.4 4.1 fusion.2
  562.5 8.7 %multiply_add_fusion = f32[2,2,4,512,128]{4,3,2,1,0:T(8,128)} fusion(f32[2,2,4,512,128]{4,3,2,1,0:T(8,128)} %get-tuple-element.360, f32[2,2,4,512]{3,2,1,0:T(4,128)S(1)} %bitcast.76, f32[2,2,512,4,512]{4,2,3,1,0:T(8,128)S(1)} %get-tuple-element.437, f32[2,2,4,512]{3,2,1,0:T(4,128)S(1)} %max.5, pred[2,512,512]{1,2,0:T(8,128)(4,1)S(1)} %broadcast_compare_fusion, ...), kind=kOutput, calls=%fused_computation.7 | convolution fusion | flops 1096810496 | bytes 26279940 | tf_op jit(solution)/shard_map/while/body/eval_jaxpr/cond/branch_0_fun/shgqk,skhd->shgqd/dot_general | solution.py:105
  572.8 17.9 %conditional.2 = (f32[2,2,4,512]{3,2,1,0:T(4,128)S(1)}, f32[2,2,4,512]{3,2,1,0:T(4,128)S(1)}, f32[2,2,4,512,128]{4,3,2,1,0:T(8,128)}) conditional(s32[]{:T(128)} %convert_element_type.85, (s32[2,512]{1,0:T(2,128)S(1)}, s32[2,512]{1,0:T(2,128)S(1)}, s32[]{:T(128)}, bf16[2,4096,2,128]{3,1,2,0:T(8,128)(2,1)}, bf16[2,2,4,512,128]{4,3,2,1,0:T(8,128)(2,1)}, ...), branch_computations={%region_7.9_spmd, %region_10.10_spmd} | conditional | flops 2204647424 | bytes 64430148 | solution.py:113
  573.2 4.7 fusion
  577.9 4.1 fusion.2
  582.0 8.7 %multiply_add_fusion = f32[2,2,4,512,128]{4,3,2,1,0:T(8,128)} fusion(f32[2,2,4,512,128]{4,3,2,1,0:T(8,128)} %get-tuple-element.360, f32[2,2,4,512]{3,2,1,0:T(4,128)S(1)} %bitcast.76, f32[2,2,512,4,512]{4,2,3,1,0:T(8,128)S(1)} %get-tuple-element.437, f32[2,2,4,512]{3,2,1,0:T(4,128)S(1)} %max.5, pred[2,512,512]{1,2,0:T(8,128)(4,1)S(1)} %broadcast_compare_fusion, ...), kind=kOutput, calls=%fused_computation.7 | convolution fusion | flops 1096810496 | bytes 26279940 | tf_op jit(solution)/shard_map/while/body/eval_jaxpr/cond/branch_0_fun/shgqk,skhd->shgqd/dot_general | solution.py:105
  592.3 17.9 %conditional.2 = (f32[2,2,4,512]{3,2,1,0:T(4,128)S(1)}, f32[2,2,4,512]{3,2,1,0:T(4,128)S(1)}, f32[2,2,4,512,128]{4,3,2,1,0:T(8,128)}) conditional(s32[]{:T(128)} %convert_element_type.85, (s32[2,512]{1,0:T(2,128)S(1)}, s32[2,512]{1,0:T(2,128)S(1)}, s32[]{:T(128)}, bf16[2,4096,2,128]{3,1,2,0:T(8,128)(2,1)}, bf16[2,2,4,512,128]{4,3,2,1,0:T(8,128)(2,1)}, ...), branch_computations={%region_7.9_spmd, %region_10.10_spmd} | conditional | flops 2204647424 | bytes 64430148 | solution.py:113
  592.7 4.8 fusion
  597.5 4.1 fusion.2
  601.7 8.6 multiply_add_fusion
  611.9 17.8 %conditional.2 = (f32[2,2,4,512]{3,2,1,0:T(4,128)S(1)}, f32[2,2,4,512]{3,2,1,0:T(4,128)S(1)}, f32[2,2,4,512,128]{4,3,2,1,0:T(8,128)}) conditional(s32[]{:T(128)} %convert_element_type.85, (s32[2,512]{1,0:T(2,128)S(1)}, s32[2,512]{1,0:T(2,128)S(1)}, s32[]{:T(128)}, bf16[2,4096,2,128]{3,1,2,0:T(8,128)(2,1)}, bf16[2,2,4,512,128]{4,3,2,1,0:T(8,128)(2,1)}, ...), branch_computations={%region_7.9_spmd, %region_10.10_spmd} | conditional | flops 2204647424 | bytes 64430148 | solution.py:113
  612.3 4.7 fusion
  617.0 4.1 fusion.2
  621.1 8.6 multiply_add_fusion
  631.4 17.8 %conditional.2 = (f32[2,2,4,512]{3,2,1,0:T(4,128)S(1)}, f32[2,2,4,512]{3,2,1,0:T(4,128)S(1)}, f32[2,2,4,512,128]{4,3,2,1,0:T(8,128)}) conditional(s32[]{:T(128)} %convert_element_type.85, (s32[2,512]{1,0:T(2,128)S(1)}, s32[2,512]{1,0:T(2,128)S(1)}, s32[]{:T(128)}, bf16[2,4096,2,128]{3,1,2,0:T(8,128)(2,1)}, bf16[2,2,4,512,128]{4,3,2,1,0:T(8,128)(2,1)}, ...), branch_computations={%region_7.9_spmd, %region_10.10_spmd} | conditional | flops 2204647424 | bytes 64430148 | solution.py:113
  631.7 4.7 fusion
  636.5 4.1 fusion.2
  640.6 8.6 multiply_add_fusion
  650.8 17.9 %conditional.2 = (f32[2,2,4,512]{3,2,1,0:T(4,128)S(1)}, f32[2,2,4,512]{3,2,1,0:T(4,128)S(1)}, f32[2,2,4,512,128]{4,3,2,1,0:T(8,128)}) conditional(s32[]{:T(128)} %convert_element_type.85, (s32[2,512]{1,0:T(2,128)S(1)}, s32[2,512]{1,0:T(2,128)S(1)}, s32[]{:T(128)}, bf16[2,4096,2,128]{3,1,2,0:T(8,128)(2,1)}, bf16[2,2,4,512,128]{4,3,2,1,0:T(8,128)(2,1)}, ...), branch_computations={%region_7.9_spmd, %region_10.10_spmd} | conditional | flops 2204647424 | bytes 64430148 | solution.py:113
  651.2 4.7 fusion
  655.9 4.1 fusion.2
  660.0 8.7 %multiply_add_fusion = f32[2,2,4,512,128]{4,3,2,1,0:T(8,128)} fusion(f32[2,2,4,512,128]{4,3,2,1,0:T(8,128)} %get-tuple-element.360, f32[2,2,4,512]{3,2,1,0:T(4,128)S(1)} %bitcast.76, f32[2,2,512,4,512]{4,2,3,1,0:T(8,128)S(1)} %get-tuple-element.437, f32[2,2,4,512]{3,2,1,0:T(4,128)S(1)} %max.5, pred[2,512,512]{1,2,0:T(8,128)(4,1)S(1)} %broadcast_compare_fusion, ...), kind=kOutput, calls=%fused_computation.7 | convolution fusion | flops 1096810496 | bytes 26279940 | tf_op jit(solution)/shard_map/while/body/eval_jaxpr/cond/branch_0_fun/shgqk,skhd->shgqd/dot_general | solution.py:105
  676.1 26.4 %convolution_convert_fusion = bf16[1024,8192]{1,0:T(8,128)(2,1)} fusion(bf16[1024,1024]{1,0:T(8,128)(2,1)} %reshape.213, bf16[1024,8192]{1,0:T(8,128)(2,1)} %all-gather.20.cloned.1.call-done), kind=kOutput, calls=%fused_computation.41 | convolution fusion | flops 17188257792 | bytes 35651584 | tf_op jit(solution)/shard_map/dot_general | solution.py:120
  702.6 152.7 %reduce-scatter.2.cloned.1.call-done = bf16[1024,2048]{1,0:T(8,128)(2,1)} async-done(((bf16[1024,8192]{1,0:T(8,128)(2,1)}), bf16[1024,2048]{1,0:T(8,128)(2,1)}) %reduce-scatter.2.cloned.1.call-update) | async-done | bytes 4194320 | tf_op jit(solution)/shard_map/reduce_scatter | solution.py:125
  (116 shorter events, 36.3 us)
Async XLA Ops:
  6.5 2.9 copy-start.1
  6.5 52.0 %all-gather.10.cloned.1.call-start = ((), (), s32[]{:S(2)}) async-start(), calls=%async_computation.2 | async-start | bytes 4718592 | tf_op jit(solution)/shard_map/all_gather | solution.py:62
  7.3 209.3 %all-gather.8.cloned.1.call-start = ((), (), s32[]{:S(2)}) async-start(), calls=%async_computation.1 | async-start | bytes 20971520 | tf_op jit(solution)/shard_map/all_gather | solution.py:50
  8.0 257.0 %all-gather.16.cloned.1.call-start = ((), (), s32[]{:S(2)}) async-start(), calls=%async_computation.5 | async-start | bytes 4718592 | tf_op jit(solution)/shard_map/all_gather | solution.py:63
  8.7 407.7 %all-gather.14.cloned.1.call-start = ((), (), s32[]{:S(2)}) async-start(), calls=%async_computation.4 | async-start | bytes 18874368 | tf_op jit(solution)/shard_map/all_gather | solution.py:61
  9.3 460.5 %all-gather.12.cloned.1.call-start = ((), (), s32[]{:S(2)}) async-start(), calls=%async_computation.3 | async-start | bytes 4718592 | tf_op jit(solution)/shard_map/all_gather | solution.py:80
  64.9 159.1 %copy-start.2 = (f32[8192]{0:T(1024)S(1)}, f32[8192]{0:T(1024)}, u32[]{:S(2)}) copy-start(f32[8192]{0:T(1024)} %param.12) | copy-start | bytes 98308
  216.5 7.5 copy-start
  234.1 276.0 %all-gather.18.cloned.1.call-start = ((), (), s32[]{:S(2)}) async-start(), calls=%async_computation.6 | async-start | bytes 4718592 | tf_op jit(solution)/shard_map/all_gather | solution.py:81
  284.1 392.1 %all-gather.20.cloned.1.call-start = ((), (), s32[]{:S(2)}) async-start(), calls=%async_computation.7 | async-start | bytes 18874368 | tf_op jit(solution)/shard_map/all_gather | solution.py:122
  284.8 570.4 %reduce-scatter.2.cloned.1.call-start = ((), (), s32[]{:S(2)}) async-start(), calls=%async_computation.8 | async-start | bytes 20971520 | tf_op jit(solution)/shard_map/reduce_scatter | solution.py:125
Sparse Core Ops, SparseCore 0:
  8.9 49.5 all-gather.9
  60.4 156.0 all-gather.7
  218.1 46.8 all-gather.15
  266.5 149.8 all-gather.13
  417.9 45.0 all-gather.11
  464.4 45.6 all-gather.17
  511.7 149.8 all-gather.19
  702.7 152.5 reduce-scatter.1
where the time goes:
time: 864 us; the launch traced here: 862 us
  waiting for transfers between devices  552 us (64%)
  matrix products  177 us (20%)
  other arithmetic  62 us (7%)
  local copies, waits for them, and re-layouts  51.1 us (6%)
  between operations  13.6 us (2%)
    reduce_scatter x1, waiting for transfers between devices, per_device(): lax.psum_scatter(terms.astype(jnp.bfloat16), 'tp', scatter_dimension=1, t...  153 us
    all_gather x1, waiting for transfers between devices, per_device(): whole = lax.all_gather(tokens, 'tp', axis=2, tiled=True)  152 us
    all_gather x1, waiting for transfers between devices, per_device(): lax.all_gather(w_query, 'ctx', axis=0, tiled=True)  131 us
    dot_general x8, matrix products, update(): jnp.einsum('shgqk,skhd->shgqd', weights.astype(jnp.bfloat16), value_block...  69.1 us
    all_gather x1, waiting for transfers between devices, per_device(): lax.all_gather(w_key, 'ctx', axis=0, tiled=True)  48 us
    dot_general x3, matrix products, per_device(): jnp.dot(normed, piece, preferred_element_type=jnp.float32)  44.1 us
    dot_general x8, matrix products, update(): jnp.einsum('shgqd,skhd->shgqk', query, key_block, preferred_element_type=...  37.6 us
    dot_general x3, local copies, waits for them, and re-layouts, per_device(): jnp.dot(normed, piece, preferred_element_type=jnp.float32)  34.1 us
  transfers between devices with their start and end apart: 8, of which 6 were waited for; matrix products, arithmetic and copies ran while one was open for 31% of the time, Pallas kernels for 0%

commit v1 on v0

--- a/solution.py
+++ b/solution.py
@@ -47,7 +47,7 @@
     total_rows = sequence_batch * rows_dev
     factor = 1.0 / math.sqrt(head_size)
     rank = lax.axis_index("ctx")
-    whole = lax.all_gather(tokens, "tp", axis=2, tiled=True)
+    whole = jnp.concatenate(lax.all_gather(tokens, "tp"), axis=2)
     normed = normalize(whole.reshape(total_rows, whole.shape[2]), norm_gain)
     query_pos = positions_of(span_order, rank * rows_dev, rows_dev, block_rows)
     latest = jnp.max(query_pos, axis=1)

time: 864 us -> 865 us (level)
  waiting for transfers between devices: 552 us -> 476 us
  local copies, waits for them, and re-layouts: 51.1 us -> 123 us
    convert_element_type x0 -> x2, local copies, waits for them, and re-layouts: none -> 68 us  [normalize(): return (wide * factor * norm_gain).astype(jnp.bfloat16)]
    all_gather x1, waiting for transfers between devices: 131 us -> 86.5 us  [per_device(): lax.all_gather(w_query, 'ctx', axis=0, tiled=True)]
    all_gather x1, waiting for transfers between devices: 30.9 us -> 0.02 us  [per_device(): lax.all_gather(value_weight, 'ctx', axis=0, tiled=True)]
  transfers between devices with their start and end apart: 8 -> 8, of which waited for: 6 -> 5; matrix products, arithmetic and copies ran while one was open for 31% -> 39% of each run, Pallas kernels for 0% -> 0%
where the time goes in v1:
time: 865 us; the launch traced here: 862 us
  waiting for transfers between devices  476 us (55%)
  matrix products  175 us (20%)
  local copies, waits for them, and re-layouts  123 us (14%)
  other arithmetic  67.6 us (8%)
  between operations  13.6 us (2%)
    reduce_scatter x1, waiting for transfers between devices, per_device(): lax.psum_scatter(terms.astype(jnp.bfloat16), 'tp', scatter_dimension=1, t...  153 us
    all_gather x1, waiting for transfers between devices, per_device(): whole = jnp.concatenate(lax.all_gather(tokens, 'tp'), axis=2)  152 us
    all_gather x1, waiting for transfers between devices, per_device(): lax.all_gather(w_query, 'ctx', axis=0, tiled=True)  86.5 us
    dot_general x8, matrix products, update(): jnp.einsum('shgqk,skhd->shgqd', weights.astype(jnp.bfloat16), value_block...  69.1 us
    convert_element_type x2, local copies, waits for them, and re-layouts, normalize(): return (wide * factor * norm_gain).astype(jnp.bfloat16)  68 us
    all_gather x1, waiting for transfers between devices, per_device(): lax.all_gather(w_key, 'ctx', axis=0, tiled=True)  48 us
    dot_general x3, matrix products, per_device(): jnp.dot(normed, piece, preferred_element_type=jnp.float32)  41.7 us
    dot_general x8, matrix products, update(): jnp.einsum('shgqd,skhd->shgqk', query, key_block, preferred_element_type=...  37.6 us
  transfers between devices with their start and end apart: 8, of which 5 were waited for; matrix products, arithmetic and copies ran while one was open for 39% of the time, Pallas kernels for 0%

profile of v1, /device:TPU:0, one launch (start us, length us, event | category | flops | bytes accessed | tf_op | source)
XLA Modules:
  0.0 862.1 jit_solution(6097449967442795863)
XLA Ops:
  10.6 48.0 %all-gather.9.cloned.1.call-done = bf16[8192,256]{1,0:T(8,128)(2,1)} async-done(((bf16[1024,256]{1,0:T(8,128)(2,1)}), bf16[8192,256]{1,0:T(8,128)(2,1)}) %all-gather.9.cloned.1.call-update) | async-done | bytes 4194320 | tf_op jit(solution)/shard_map/all_gather | solution.py:62
  58.6 6.3 copy.36
  64.9 151.6 %all-gather.21.cloned.1.call-done = bf16[8,512,2048]{2,1,0:T(8,128)(2,1)} async-done(((bf16[2,512,2048]{2,1,0:T(8,128)(2,1)}), bf16[8,512,2048]{2,1,0:T(8,128)(2,1)}) %all-gather.21.cloned.1.call-update) | async-done | bytes 16777232 | tf_op jit(solution)/shard_map/all_gather | solution.py:50
  216.5 7.5 fusion.21
  227.9 5.6 fusion.24
  233.5 40.2 %copy.35 = bf16[2,512,4,2048]{3,2,1,0:T(4,128)(2,1)} copy(bf16[2,512,4,2048]{3,1,0,2:T(8,128)(2,1)S(1)} %fusion.24) | data formatting | bytes 33554432 | tf_op jit(solution)/shard_map/convert_element_type | solution.py:16
  273.7 27.9 %reshape.244 = bf16[2,512,8192,1]{2,1,0,3:T(8,128)(2,1)} reshape(bf16[2,512,4,2048]{3,2,1,0:T(4,128)(2,1)} %copy.35) | data formatting | bytes 33554432 | tf_op jit(solution)/shard_map/convert_element_type | solution.py:16
  301.5 9.7 %fusion.29 = f32[2,512,2,128]{1,3,2,0:T(8,128)S(1)} fusion(bf16[2,128,8192,1]{2,1,0,3:T(8,128)(2,1)} %bitcast.77, bf16[2,512,8192,1]{2,1,0,3:T(8,128)(2,1)} %reshape.244), kind=kOutput, calls=%fused_computation.45 | convolution fusion | flops 4294967296 | bytes 22020096 | tf_op jit(solution)/shard_map/dot_general | solution.py:66
  312.4 6.4 copy.40
  318.7 10.1 %fusion.32 = bf16[2,512,2,128]{3,1,2,0:T(8,128)(2,1)} fusion(bf16[2,128,8192,1]{2,1,0,3:T(8,128)(2,1)} %bitcast.78, bf16[2,512,8192,1]{2,1,0,3:T(8,128)(2,1)} %reshape.244), kind=kOutput, calls=%fused_computation.53 | convolution fusion | flops 4295229440 | bytes 21495808 | tf_op jit(solution)/shard_map/dot_general | solution.py:66
  329.9 86.5 %all-gather.13.cloned.1.call-done = bf16[8192,1024]{1,0:T(8,128)(2,1)} async-done(((bf16[1024,1024]{1,0:T(8,128)(2,1)}), bf16[8192,1024]{1,0:T(8,128)(2,1)}) %all-gather.13.cloned.1.call-update) | async-done | bytes 16777232 | tf_op jit(solution)/shard_map/all_gather | solution.py:61
  416.4 21.4 %copy.37 = bf16[1024,8192]{1,0:T(8,128)(2,1)} copy(bf16[1024,8192]{0,1:T(8,128)(2,1)} %bitcast.71) | data formatting | bytes 33554432 | tf_op jit(solution)/shard_map/dot_general | solution.py:66
  437.8 22.0 %fusion.27 = f32[2,512,8,128]{1,3,2,0:T(8,128)S(1)} fusion(bf16[8,128,8192,1]{2,1,0,3:T(8,128)(2,1)} %bitcast.72, bf16[2,512,8192,1]{2,1,0,3:T(8,128)(2,1)} %reshape.244), kind=kOutput, calls=%fused_computation.43 | convolution fusion | flops 17179869184 | bytes 37748736 | tf_op jit(solution)/shard_map/dot_general | solution.py:66
  469.4 6.4 copy.41
  475.8 34.3 %all-gather.17.cloned.1.call-done = bf16[2,4096,2,128]{3,1,2,0:T(8,128)(2,1)} async-done(((bf16[2,512,2,128]{3,1,2,0:T(8,128)(2,1)}), bf16[2,4096,2,128]{3,1,2,0:T(8,128)(2,1)}) %all-gather.17.cloned.1.call-update) | async-done | bytes 4194320 | tf_op jit(solution)/shard_map/all_gather | solution.py:81
  512.6 156.1 %while.19 = (s32[]{:T(128)}, f32[2,2,4,512]{3,2,1,0:T(4,128)S(1)}, f32[2,2,4,512]{3,2,1,0:T(4,128)S(1)}, f32[2,2,4,512,128]{4,3,2,1,0:T(8,128)}, s32[2,16]{1,0:T...) while((s32[]{:T(128)}, f32[2,2,4,512]{3,2,1,0:T(4,128)S(1)}, ...), condition=%wide.region_11.12_spmd, body=%wide.region_3.11_spmd.sunk | while | flops 2204700672 | bytes 64532936 | solution.py:117
  514.2 17.9 %conditional.2 = (f32[2,2,4,512]{3,2,1,0:T(4,128)S(1)}, f32[2,2,4,512]{3,2,1,0:T(4,128)S(1)}, f32[2,2,4,512,128]{4,3,2,1,0:T(8,128)}) conditional(s32[]{:T(128)} %convert_element_type.96, (s32[2,512]{1,0:T(2,128)S(1)}, s32[2,512]{1,0:T(2,128)S(1)}, s32[]{:T(128)}, bf16[2,4096,2,128]{3,1,2,0:T(8,128)(2,1)}, bf16[2,2,4,512,128]{4,3,2,1,0:T(8,128)(2,1)}, ...), branch_computations={%region_7.9_spmd, %region_10.10_spmd} | conditional | flops 2204647424 | bytes 64430148 | solution.py:113
  514.6 4.7 fusion
  519.3 4.1 fusion.2
  523.4 8.7 %multiply_add_fusion = f32[2,2,4,512,128]{4,3,2,1,0:T(8,128)} fusion(f32[2,2,4,512,128]{4,3,2,1,0:T(8,128)} %get-tuple-element.360, f32[2,2,4,512]{3,2,1,0:T(4,128)S(1)} %bitcast.84, f32[2,2,512,4,512]{4,2,3,1,0:T(8,128)S(1)} %get-tuple-element.447, f32[2,2,4,512]{3,2,1,0:T(4,128)S(1)} %max.5, pred[2,512,512]{1,2,0:T(8,128)(4,1)S(1)} %broadcast_compare_fusion, ...), kind=kOutput, calls=%fused_computation.7 | convolution fusion | flops 1096810496 | bytes 26279940 | tf_op jit(solution)/shard_map/while/body/eval_jaxpr/cond/branch_0_fun/shgqk,skhd->shgqd/dot_general | solution.py:105
  533.8 17.9 %conditional.2 = (f32[2,2,4,512]{3,2,1,0:T(4,128)S(1)}, f32[2,2,4,512]{3,2,1,0:T(4,128)S(1)}, f32[2,2,4,512,128]{4,3,2,1,0:T(8,128)}) conditional(s32[]{:T(128)} %convert_element_type.96, (s32[2,512]{1,0:T(2,128)S(1)}, s32[2,512]{1,0:T(2,128)S(1)}, s32[]{:T(128)}, bf16[2,4096,2,128]{3,1,2,0:T(8,128)(2,1)}, bf16[2,2,4,512,128]{4,3,2,1,0:T(8,128)(2,1)}, ...), branch_computations={%region_7.9_spmd, %region_10.10_spmd} | conditional | flops 2204647424 | bytes 64430148 | solution.py:113
  534.1 4.7 fusion
  538.9 4.1 fusion.2
  543.0 8.7 %multiply_add_fusion = f32[2,2,4,512,128]{4,3,2,1,0:T(8,128)} fusion(f32[2,2,4,512,128]{4,3,2,1,0:T(8,128)} %get-tuple-element.360, f32[2,2,4,512]{3,2,1,0:T(4,128)S(1)} %bitcast.84, f32[2,2,512,4,512]{4,2,3,1,0:T(8,128)S(1)} %get-tuple-element.447, f32[2,2,4,512]{3,2,1,0:T(4,128)S(1)} %max.5, pred[2,512,512]{1,2,0:T(8,128)(4,1)S(1)} %broadcast_compare_fusion, ...), kind=kOutput, calls=%fused_computation.7 | convolution fusion | flops 1096810496 | bytes 26279940 | tf_op jit(solution)/shard_map/while/body/eval_jaxpr/cond/branch_0_fun/shgqk,skhd->shgqd/dot_general | solution.py:105
  553.3 17.9 %conditional.2 = (f32[2,2,4,512]{3,2,1,0:T(4,128)S(1)}, f32[2,2,4,512]{3,2,1,0:T(4,128)S(1)}, f32[2,2,4,512,128]{4,3,2,1,0:T(8,128)}) conditional(s32[]{:T(128)} %convert_element_type.96, (s32[2,512]{1,0:T(2,128)S(1)}, s32[2,512]{1,0:T(2,128)S(1)}, s32[]{:T(128)}, bf16[2,4096,2,128]{3,1,2,0:T(8,128)(2,1)}, bf16[2,2,4,512,128]{4,3,2,1,0:T(8,128)(2,1)}, ...), branch_computations={%region_7.9_spmd, %region_10.10_spmd} | conditional | flops 2204647424 | bytes 64430148 | solution.py:113
  553.7 4.7 fusion
  558.4 4.1 fusion.2
  562.5 8.7 %multiply_add_fusion = f32[2,2,4,512,128]{4,3,2,1,0:T(8,128)} fusion(f32[2,2,4,512,128]{4,3,2,1,0:T(8,128)} %get-tuple-element.360, f32[2,2,4,512]{3,2,1,0:T(4,128)S(1)} %bitcast.84, f32[2,2,512,4,512]{4,2,3,1,0:T(8,128)S(1)} %get-tuple-element.447, f32[2,2,4,512]{3,2,1,0:T(4,128)S(1)} %max.5, pred[2,512,512]{1,2,0:T(8,128)(4,1)S(1)} %broadcast_compare_fusion, ...), kind=kOutput, calls=%fused_computation.7 | convolution fusion | flops 1096810496 | bytes 26279940 | tf_op jit(solution)/shard_map/while/body/eval_jaxpr/cond/branch_0_fun/shgqk,skhd->shgqd/dot_general | solution.py:105
  572.8 17.9 %conditional.2 = (f32[2,2,4,512]{3,2,1,0:T(4,128)S(1)}, f32[2,2,4,512]{3,2,1,0:T(4,128)S(1)}, f32[2,2,4,512,128]{4,3,2,1,0:T(8,128)}) conditional(s32[]{:T(128)} %convert_element_type.96, (s32[2,512]{1,0:T(2,128)S(1)}, s32[2,512]{1,0:T(2,128)S(1)}, s32[]{:T(128)}, bf16[2,4096,2,128]{3,1,2,0:T(8,128)(2,1)}, bf16[2,2,4,512,128]{4,3,2,1,0:T(8,128)(2,1)}, ...), branch_computations={%region_7.9_spmd, %region_10.10_spmd} | conditional | flops 2204647424 | bytes 64430148 | solution.py:113
  573.2 4.7 fusion
  577.9 4.1 fusion.2
  582.0 8.7 %multiply_add_fusion = f32[2,2,4,512,128]{4,3,2,1,0:T(8,128)} fusion(f32[2,2,4,512,128]{4,3,2,1,0:T(8,128)} %get-tuple-element.360, f32[2,2,4,512]{3,2,1,0:T(4,128)S(1)} %bitcast.84, f32[2,2,512,4,512]{4,2,3,1,0:T(8,128)S(1)} %get-tuple-element.447, f32[2,2,4,512]{3,2,1,0:T(4,128)S(1)} %max.5, pred[2,512,512]{1,2,0:T(8,128)(4,1)S(1)} %broadcast_compare_fusion, ...), kind=kOutput, calls=%fused_computation.7 | convolution fusion | flops 1096810496 | bytes 26279940 | tf_op jit(solution)/shard_map/while/body/eval_jaxpr/cond/branch_0_fun/shgqk,skhd->shgqd/dot_general | solution.py:105
  592.3 17.9 %conditional.2 = (f32[2,2,4,512]{3,2,1,0:T(4,128)S(1)}, f32[2,2,4,512]{3,2,1,0:T(4,128)S(1)}, f32[2,2,4,512,128]{4,3,2,1,0:T(8,128)}) conditional(s32[]{:T(128)} %convert_element_type.96, (s32[2,512]{1,0:T(2,128)S(1)}, s32[2,512]{1,0:T(2,128)S(1)}, s32[]{:T(128)}, bf16[2,4096,2,128]{3,1,2,0:T(8,128)(2,1)}, bf16[2,2,4,512,128]{4,3,2,1,0:T(8,128)(2,1)}, ...), branch_computations={%region_7.9_spmd, %region_10.10_spmd} | conditional | flops 2204647424 | bytes 64430148 | solution.py:113
  592.7 4.8 fusion
  597.5 4.1 fusion.2
  601.6 8.6 multiply_add_fusion
  611.9 17.8 %conditional.2 = (f32[2,2,4,512]{3,2,1,0:T(4,128)S(1)}, f32[2,2,4,512]{3,2,1,0:T(4,128)S(1)}, f32[2,2,4,512,128]{4,3,2,1,0:T(8,128)}) conditional(s32[]{:T(128)} %convert_element_type.96, (s32[2,512]{1,0:T(2,128)S(1)}, s32[2,512]{1,0:T(2,128)S(1)}, s32[]{:T(128)}, bf16[2,4096,2,128]{3,1,2,0:T(8,128)(2,1)}, bf16[2,2,4,512,128]{4,3,2,1,0:T(8,128)(2,1)}, ...), branch_computations={%region_7.9_spmd, %region_10.10_spmd} | conditional | flops 2204647424 | bytes 64430148 | solution.py:113
  612.3 4.7 fusion
  617.0 4.1 fusion.2
  621.1 8.6 multiply_add_fusion
  631.3 17.8 %conditional.2 = (f32[2,2,4,512]{3,2,1,0:T(4,128)S(1)}, f32[2,2,4,512]{3,2,1,0:T(4,128)S(1)}, f32[2,2,4,512,128]{4,3,2,1,0:T(8,128)}) conditional(s32[]{:T(128)} %convert_element_type.96, (s32[2,512]{1,0:T(2,128)S(1)}, s32[2,512]{1,0:T(2,128)S(1)}, s32[]{:T(128)}, bf16[2,4096,2,128]{3,1,2,0:T(8,128)(2,1)}, bf16[2,2,4,512,128]{4,3,2,1,0:T(8,128)(2,1)}, ...), branch_computations={%region_7.9_spmd, %region_10.10_spmd} | conditional | flops 2204647424 | bytes 64430148 | solution.py:113
  631.7 4.7 fusion
  640.6 8.6 multiply_add_fusion
  650.8 17.9 %conditional.2 = (f32[2,2,4,512]{3,2,1,0:T(4,128)S(1)}, f32[2,2,4,512]{3,2,1,0:T(4,128)S(1)}, f32[2,2,4,512,128]{4,3,2,1,0:T(8,128)}) conditional(s32[]{:T(128)} %convert_element_type.96, (s32[2,512]{1,0:T(2,128)S(1)}, s32[2,512]{1,0:T(2,128)S(1)}, s32[]{:T(128)}, bf16[2,4096,2,128]{3,1,2,0:T(8,128)(2,1)}, bf16[2,2,4,512,128]{4,3,2,1,0:T(8,128)(2,1)}, ...), branch_computations={%region_7.9_spmd, %region_10.10_spmd} | conditional | flops 2204647424 | bytes 64430148 | solution.py:113
  651.2 4.7 fusion
  660.0 8.7 %multiply_add_fusion = f32[2,2,4,512,128]{4,3,2,1,0:T(8,128)} fusion(f32[2,2,4,512,128]{4,3,2,1,0:T(8,128)} %get-tuple-element.360, f32[2,2,4,512]{3,2,1,0:T(4,128)S(1)} %bitcast.84, f32[2,2,512,4,512]{4,2,3,1,0:T(8,128)S(1)} %get-tuple-element.447, f32[2,2,4,512]{3,2,1,0:T(4,128)S(1)} %max.5, pred[2,512,512]{1,2,0:T(8,128)(4,1)S(1)} %broadcast_compare_fusion, ...), kind=kOutput, calls=%fused_computation.7 | convolution fusion | flops 1096810496 | bytes 26279940 | tf_op jit(solution)/shard_map/while/body/eval_jaxpr/cond/branch_0_fun/shgqk,skhd->shgqd/dot_general | solution.py:105
  676.1 26.4 %convolution_convert_fusion = bf16[1024,8192]{1,0:T(8,128)(2,1)} fusion(bf16[1024,1024]{1,0:T(8,128)(2,1)} %reshape.238, bf16[1024,8192]{1,0:T(8,128)(2,1)} %all-gather.19.cloned.1.call-done), kind=kOutput, calls=%fused_computation.47 | convolution fusion | flops 17188257792 | bytes 35651584 | tf_op jit(solution)/shard_map/dot_general | solution.py:120
  702.5 152.7 %reduce-scatter.2.cloned.1.call-done = bf16[1024,2048]{1,0:T(8,128)(2,1)} async-done(((bf16[1024,8192]{1,0:T(8,128)(2,1)}), bf16[1024,2048]{1,0:T(8,128)(2,1)}) %reduce-scatter.2.cloned.1.call-update) | async-done | bytes 4194320 | tf_op jit(solution)/shard_map/reduce_scatter | solution.py:125
  (120 shorter events, 48.4 us)
Async XLA Ops:
  6.5 2.8 copy-start.2
  6.5 2.9 copy-start.1
  6.5 52.0 %all-gather.9.cloned.1.call-start = ((), (), s32[]{:S(2)}) async-start(), calls=%async_computation.1 | async-start | bytes 4718592 | tf_op jit(solution)/shard_map/all_gather | solution.py:62
  7.3 209.3 %all-gather.21.cloned.1.call-start = ((), (), s32[]{:S(2)}) async-start(), calls=%async_computation.8 | async-start | bytes 20971520 | tf_op jit(solution)/shard_map/all_gather | solution.py:50
  8.0 304.3 %all-gather.15.cloned.1.call-start = ((), (), s32[]{:S(2)}) async-start(), calls=%async_computation.4 | async-start | bytes 4718592 | tf_op jit(solution)/shard_map/all_gather | solution.py:63
  8.7 407.7 %all-gather.13.cloned.1.call-start = ((), (), s32[]{:S(2)}) async-start(), calls=%async_computation.3 | async-start | bytes 18874368 | tf_op jit(solution)/shard_map/all_gather | solution.py:61
  9.3 460.1 %all-gather.11.cloned.1.call-start = ((), (), s32[]{:S(2)}) async-start(), calls=%async_computation.2 | async-start | bytes 4718592 | tf_op jit(solution)/shard_map/all_gather | solution.py:80
  216.5 11.4 %copy-start = (bf16[8,512,2048]{2,1,0:T(8,128)(2,1)S(1)}, bf16[8,512,2048]{2,1,0:T(8,128)(2,1)}, u32[]{:S(2)}) copy-start(bf16[8,512,2048]{2,1,0:T(8,128)(2,1)} %all-gather.21.cloned.1.call-done) | copy-start | bytes 50331652
  312.3 197.8 %all-gather.17.cloned.1.call-start = ((), (), s32[]{:S(2)}) async-start(), calls=%async_computation.5 | async-start | bytes 4718592 | tf_op jit(solution)/shard_map/all_gather | solution.py:81
  328.8 347.3 %all-gather.19.cloned.1.call-start = ((), (), s32[]{:S(2)}) async-start(), calls=%async_computation.6 | async-start | bytes 18874368 | tf_op jit(solution)/shard_map/all_gather | solution.py:122
  329.6 525.6 %reduce-scatter.2.cloned.1.call-start = ((), (), s32[]{:S(2)}) async-start(), calls=%async_computation.7 | async-start | bytes 20971520 | tf_op jit(solution)/shard_map/reduce_scatter | solution.py:125
Sparse Core Ops, SparseCore 0:
  8.9 49.5 all-gather.8
  60.4 156.0 all-gather.20
  218.1 46.8 all-gather.14
  266.5 149.8 all-gather.12
  417.9 45.0 all-gather.10
  464.4 45.6 all-gather.16
  511.7 149.8 all-gather.18
  702.7 152.5 reduce-scatter.1
